TPU v7x, 32 devices: a whole 2x2x4 slice. The times are simulated.
32 devices in a mesh: bank: 4 (over y, x), zero: 8 (over z, core).
Axes of the slice: x: 2, y: 2, z: 4, core: 2. Of those that a mesh axis runs over, the one named last changes fastest.
Arguments:
- master_gate: float32 [64, 2048, 1024], P('bank', 'zero'), may hold values from -0.1875 to 0.1875
- master_up: float32 [64, 2048, 1024], P('bank', 'zero'), may hold values from -0.1875 to 0.1875
- master_down: float32 [64, 1024, 2048], P('bank', None, 'zero'), may hold values from -0.25 to 0.25
- router_weight: float32 [2048, 64], P('zero', 'bank'), may hold values from -0.125 to 0.125
- router_gain: float32 [2048], P('zero'), may hold values from 0.25 to 1.75
Outputs:
- final_gate: bfloat16 [64, 2048, 1024], P('bank', None, 'zero')
- final_up: bfloat16 [64, 2048, 1024], P('bank', None, 'zero')
- final_down: bfloat16 [64, 1024, 2048], P('bank', 'zero')
- scale_gate: float32 [64, 1024], P('bank', 'zero')
- scale_up: float32 [64, 1024], P('bank', 'zero')
- scale_down: float32 [64, 1024], P('bank', 'zero')
- serve_router: bfloat16 [2048, 64], replicated
All inputs are finite; a program needn't handle non-finite values.
Results may differ from a plain program's by a relative error of at most 0.0085.
Values may be sent and summed in bfloat16 or wider, within the bound.
No kernel may reach another device: no remote copies, remote signals or barrier semaphores. Data moves between devices by JAX's collectives and lax.ppermute only.
A program may use at most 192 MiB of HBM per device.

v0:
```python
import functools

import jax
import jax.numpy as jnp
from jax import lax
from jax.experimental import pallas as pl
from jax.experimental.pallas import tpu as pltpu
from jax.sharding import PartitionSpec as P


LANES = 128
ROWS = 16
LARGE, SMALL = 47 * 2**20, 16 * 2**20
PARAMS = pltpu.CompilerParams(dimension_semantics=("arbitrary",), vmem_limit_bytes=SMALL)


def piece(axis, place, size):
    at = pl.ds(pl.multiple_of(place * size, size), size)
    return (slice(None), at, slice(None)) if axis == 1 else (slice(None), slice(None), at)


def step_of(first, count):
    return next(size for size in (4, 3, 2, 1) if first % size == 0 and count % size == 0)


def narrow_kernel(axis, x_ref, *out_refs):
    me = lax.axis_index("zero")
    for k, out_ref in enumerate(out_refs):
        at = piece(axis, me ^ k, out_ref.shape[axis])
        out_ref[...] = x_ref[at].astype(jnp.bfloat16)


def narrow_all_kernel(axis, x_ref, out_ref):
    for k in range(out_ref.shape[0]):
        at = piece(axis, k, out_ref.shape[1 + axis])
        out_ref[k] = x_ref[at].astype(jnp.bfloat16)


def narrow(x, axis, first, count, n, single):
    shape = list(x.shape[1:])
    shape[axis - 1] //= n
    size = step_of(first, count)
    if single:
        kernel = functools.partial(narrow_all_kernel, axis)
        out_specs = pl.BlockSpec((n, size, *shape), lambda e: (0, e, 0, 0))
        out_shape = jax.ShapeDtypeStruct((n, count, *shape), jnp.bfloat16)
    else:
        kernel = functools.partial(narrow_kernel, axis)
        out_specs = [pl.BlockSpec((size, *shape), lambda e: (e, 0, 0))] * n
        out_shape = [jax.ShapeDtypeStruct((count, *shape), jnp.bfloat16)] * n
    return pl.pallas_call(
        kernel,
        grid=(count // size,),
        in_specs=[pl.BlockSpec((size, *x.shape[1:]), lambda e: (first // size + e, 0, 0))],
        out_specs=out_specs,
        out_shape=out_shape,
        compiler_params=pltpu.CompilerParams(
            dimension_semantics=("arbitrary",), vmem_limit_bytes=LARGE
        ),
    )(x)


def serve_kernel(axis, first, single, n, again, *refs):
    if single:
        parts, refs = [refs[0].at[k] for k in range(n)], refs[1:]
        places = range(n)
    else:
        parts, refs = refs[:n], refs[n:]
        me = lax.axis_index("zero")
        places = [me ^ k for k in range(n)]
    if again:
        held, refs = refs[1], refs[2:]
    out_ref, scale_ref = refs
    step = pl.program_id(0)
    if again:

        @pl.when(step == 0)
        def _():
            scale_ref[...] = held[...]

    size = out_ref.shape[0]
    for i in range(size):
        total = None
        for part in parts:
            wide = part[i].astype(jnp.float32)
            squares = jnp.sum(wide * wide, axis=axis - 1, keepdims=True)
            total = squares if total is None else total + squares
        scale = jnp.sqrt(total)
        if axis == 1:
            row = scale
        else:
            width = scale.shape[0]
            eye = lax.broadcasted_iota(jnp.int32, (width, width), 0) == lax.broadcasted_iota(
                jnp.int32, (width, width), 1
            )
            row = jnp.sum(jnp.where(eye, scale, 0.0), axis=0, keepdims=True)
        scale_ref[pl.ds(first + step * size + i, 1), :] = row
        for place, part in zip(places, parts, strict=True):
            at = (i, *piece(axis, place, part.shape[axis])[1:])
            out_ref[at] = (part[i].astype(jnp.float32) / scale).astype(jnp.bfloat16)


def serve(parts, axis, first, experts, held):
    single = not isinstance(parts, list)
    if single:
        n, count, *shape = parts.shape
        size = step_of(first, count)
        in_specs = [pl.BlockSpec((n, size, *shape), lambda e: (0, e, 0, 0))]
        parts = [parts]
    else:
        n = len(parts)
        count, *shape = parts[0].shape
        size = step_of(first, count)
        in_specs = [pl.BlockSpec((size, *shape), lambda e: (e, 0, 0))] * n
    whole = list(shape)
    whole[axis - 1] *= n
    width = shape[1] if axis == 1 else shape[0]
    full = pl.BlockSpec((experts, width), lambda e: (0, 0))
    aliases = {}
    if held is not None:
        aliases = {len(in_specs): 0}
        in_specs = in_specs + [pl.BlockSpec(memory_space=pl.ANY), full]
    return pl.pallas_call(
        functools.partial(serve_kernel, axis, first, single, n, held is not None),
        grid=(count // size,),
        in_specs=in_specs,
        out_specs=[pl.BlockSpec((size, *whole), lambda e: (first // size + e, 0, 0)), full],
        out_shape=[
            jax.ShapeDtypeStruct((experts, *whole), jnp.bfloat16),
            jax.ShapeDtypeStruct((experts, width), jnp.float32),
        ],
        input_output_aliases=aliases,
        compiler_params=PARAMS,
    )(*parts, *(held or ()))


def exchange(x, name, size, k):
    return lax.ppermute(x, name, [(i, i ^ k) for i in range(size)])


def fold_kernel(weight_ref, gain_ref, out_ref):
    out_ref[...] = (weight_ref[...] * gain_ref[...]).astype(out_ref.dtype)


def join_kernel(*refs):
    *piece_refs, out_ref = refs
    for k, piece_ref in enumerate(piece_refs):
        out_ref[k] = piece_ref[...]


def place_kernel(banks, *refs):
    *halves, out_ref = refs
    me, bank = lax.axis_index("zero"), lax.axis_index("bank")
    for j in range(banks):
        for core in range(2):
            half = halves[2 * j + core]
            count, rows, width = half.shape
            for k in range(count):
                at = (
                    pl.ds(pl.multiple_of((bank ^ j) * rows, rows), rows),
                    pl.ds(pl.multiple_of((me ^ (2 * k + core)) * width, width), width),
                )
                out_ref[at] = half[k]


def whole_call(kernel, shape, *operands):
    out = jax.ShapeDtypeStruct(shape, jnp.bfloat16)
    params = pltpu.CompilerParams(vmem_limit_bytes=SMALL)
    return pl.pallas_call(kernel, out_shape=out, compiler_params=params)(*operands)


def start_router(router_weight, router_gain, n):
    weight = router_weight.T
    mine = whole_call(fold_kernel, weight.shape, weight, router_gain[None, :])
    pieces = [mine]
    for k in range(2, n, 2):
        pieces.append(exchange(mine, "zero", n, k))
    return pieces


def finish_router(pieces, n, banks):
    rows, width = pieces[0].shape
    half = whole_call(join_kernel, (n // 2, rows, width), *pieces)
    pair = [half, exchange(half, "zero", n, 1)]
    halves = list(pair)
    for j in range(1, banks):
        for core in range(2):
            halves.append(exchange(pair[core], "bank", banks, j))
    kernel = functools.partial(place_kernel, banks)
    return whole_call(kernel, (banks * rows, n * width), *halves).T


def chunks(experts):
    small, middle = experts // 16, experts * 3 // 16
    rest = experts - small - middle
    return [
        (2, rest + middle, small, False),
        (2, rest, middle, False),
        (2, 0, rest, True),
        (1, 0, experts, False),
        (0, 0, rest, True),
        (0, rest, middle, False),
        (0, rest + middle, small, False),
    ]


def by_pieces(n, banks, masters, router_weight, router_gain):
    axes = (2, 2, 1)
    experts = masters[0].shape[0]
    arrived = []
    for tensor, first, count, single in chunks(experts):
        pieces = narrow(masters[tensor], axes[tensor], first, count, n, single)
        if single:
            pieces = lax.all_to_all(pieces, "zero", 0, 0, tiled=True)
        else:
            pieces = list(pieces)
            for k in range(1, n):
                pieces[k] = exchange(pieces[k], "zero", n, k)
        arrived.append((tensor, first, pieces))
    router = start_router(router_weight, router_gain, n)
    serve_router = finish_router(router, n, banks)
    held = [None, None, None]
    for tensor, first, pieces in arrived:
        held[tensor] = serve(pieces, 3 - axes[tensor], first, experts, held[tensor])
    finals, scales = zip(*held, strict=True)
    return (*finals, *scales, serve_router)


def by_arrays(masters, router_weight, router_gain):
    finals, scales = [], []
    for master, axis in zip(masters, (1, 1, 2), strict=True):
        whole = lax.all_to_all(
            master.astype(jnp.bfloat16), "zero", split_axis=3 - axis, concat_axis=axis, tiled=True
        ).astype(jnp.float32)
        scale = jnp.sqrt(jnp.sum(whole * whole, axis=axis))
        finals.append((whole / jnp.expand_dims(scale, axis)).astype(jnp.bfloat16))
        scales.append(scale)
    part_router = (router_weight * router_gain[:, None]).astype(jnp.bfloat16)
    row_router = lax.all_gather(part_router, "zero", axis=0, tiled=True)
    return (*finals, *scales, lax.all_gather(row_router, "bank", axis=1, tiled=True))


def power_of_two(n):
    return n & (n - 1) == 0


def fits(n, banks, masters, router_weight):
    rows, columns = router_weight
    good = power_of_two(n) and power_of_two(banks) and n > 1
    good = good and rows % LANES == 0 and columns % ROWS == 0
    for shape, axis in zip(masters, (2, 2, 1), strict=True):
        good = good and shape[axis] % (n * LANES) == 0 and shape[3 - axis] % LANES == 0
        good = good and shape[0] >= 16
    return good


def local(n, banks, master_gate, master_up, master_down, router_weight, router_gain):
    masters = (master_gate, master_up, master_down)
    if fits(n, banks, [master.shape for master in masters], router_weight.shape):
        return by_pieces(n, banks, masters, router_weight, router_gain)
    return by_arrays(masters, router_weight, router_gain)


def solution(mesh):
    in_specs = (
        P("bank", "zero", None),
        P("bank", "zero", None),
        P("bank", None, "zero"),
        P("zero", "bank"),
        P("zero"),
    )
    out_specs = (
        P("bank", None, "zero"),
        P("bank", None, "zero"),
        P("bank", "zero", None),
        P("bank", "zero"),
        P("bank", "zero"),
        P("bank", "zero"),
        P(),
    )
    n, banks = mesh.shape["zero"], mesh.shape["bank"]
    step = jax.shard_map(
        functools.partial(local, n, banks),
        mesh=mesh,
        in_specs=in_specs,
        out_specs=out_specs,
        check_vma=False,
    )

    def whole(*arguments):
        own = []
        for shape, spec in zip((a.shape for a in arguments), in_specs, strict=True):
            own.append([size // mesh.shape.get(name, 1) for size, name in zip(shape, spec, strict=True)])
        if not fits(n, banks, own[:3], own[3]):
            return step(*arguments)
        return step(*arguments)

    return whole
```

profile of v0, /device:TPU:9, one launch (start us, length us, event | category | flops | bytes accessed | tf_op | source)
XLA Modules:
  0.0 652.5 jit_solution(7370476926117248543)
XLA Ops:
  0.6 5.7 shard_map.110
  6.3 2.7 copy-done.1
  9.0 5.6 all-to-all-start
  14.6 5.3 shard_map.116
  22.5 127.5 %all-to-all-done.refs_0_ = bf16[8,12,256,128]{3,2,1,0:T(8,128)(2,1)} async-done(((bf16[8,12,256,128]{3,2,1,0:T(8,128)(2,1)}), bf16[8,12,256,128]{3,2,1,0:T(8,128)(2,1)}, u32[]{:S(2)}, u32[]{:S(2)}) %all-to-all-start) | async-done | bytes 6291488 | tf_op jit(solution)/shard_map/all_to_all | solution.py:214
  150.0 8.2 %all-to-all-start.1 = ((bf16[8,12,128,256]{3,2,1,0:T(8,128)(2,1)}), bf16[8,12,128,256]{3,2,1,0:T(8,128)(2,1)}, u32[]{:S(2)}, u32[]{:S(2)}) async-start(bf16[8,12,128,256]{3,2,1,0:T(8,128)(2,1)} %copy-done), calls=%async_computation.1 | async-start | bytes 12582912 | tf_op jit(solution)/shard_map/all_to_all | solution.py:214
  161.7 133.8 %collective-permute-done.37.refs_3_ = bf16[16,256]{1,0:T(8,128)(2,1)S(1)} collective-permute-done((bf16[16,256]{1,0:T(8,128)(2,1)S(1)}, bf16[16,256]{1,0:T(8,128)(2,1)S(1)}, u32[]{:S(2)}, u32[]{:S(2)}) %collective-permute-start.37) | collective-permute-done | bytes 8224 | tf_op jit(solution)/shard_map/ppermute | solution.py:138
  306.9 2.6 collective-permute-start.32
  309.5 8.1 %shard_map.114 = (bf16[16,256,128]{2,1,0:T(8,128)(2,1)S(1)}, bf16[16,256,128]{2,1,0:T(8,128)(2,1)S(1)}, bf16[16,256,128]{2,1,0:T(8,128)(2,1)S(1)}, bf16[16,256,1...) custom-call(f32[16,256,1024]{2,1,0:T(8,128)} %x_ref.10), custom_call_target="tpu_custom_call" | custom-call | tf_op jit(solution)/shard_map/pallas_call | solution.py:51
  325.1 2.7 collective-permute-done.34.refs_7_
  337.7 26.9 %collective-permute-start.9 = (bf16[3,256,128]{2,1,0:T(8,128)(2,1)S(1)}, bf16[3,256,128]{2,1,0:T(8,128)(2,1)S(1)}, u32[]{:S(2)}, u32[]{:S(2)}) collective-permute-start(bf16[3,256,128]{2,1,0:T(8,128)(2,1)S(1)} %get-tuple-element.72), channel_id=1, source_target_pairs={{0,3},{1,2},{2,1},{3,0},{4,7},{5,6},{6,5},{7,4},{8,11},{9,10},{10,... | collective-permute-start | bytes 589832 | tf_op jit(solution)/shard_map/ppermute | solution.py:138
  370.7 9.4 %collective-permute-done.10.refs_4_ = bf16[3,256,128]{2,1,0:T(8,128)(2,1)S(1)} collective-permute-done((bf16[3,256,128]{2,1,0:T(8,128)(2,1)S(1)}, bf16[3,256,128]{2,1,0:T(8,128)(2,1)S(1)}, u32[]{:S(2)}, u32[]{:S(2)}) %collective-permute-start.10) | collective-permute-done | bytes 196640 | tf_op jit(solution)/shard_map/ppermute | solution.py:138
  380.2 3.8 collective-permute-start.13
  384.5 7.9 %collective-permute-start.21 = (bf16[3,128,256]{2,1,0:T(8,128)(2,1)S(1)}, bf16[3,128,256]{2,1,0:T(8,128)(2,1)S(1)}, u32[]{:S(2)}, u32[]{:S(2)}) collective-permute-start(bf16[3,128,256]{2,1,0:T(8,128)(2,1)S(1)} %get-tuple-element.92), channel_id=1, source_target_pairs={{0,1},{1,0},{2,3},{3,2},{4,5},{5,4},{6,7},{7,6},{8,9},{9,8},{10,11... | collective-permute-start | bytes 589832 | tf_op jit(solution)/shard_map/ppermute | solution.py:138
  392.5 3.9 collective-permute-done.12.refs_6_
  396.3 4.6 collective-permute-done.13.refs_7_
  401.7 2.7 collective-permute-start.25
  404.4 4.3 collective-permute-done.23.refs_3_
  411.4 10.7 %collective-permute-start.27 = (bf16[3,128,256]{2,1,0:T(8,128)(2,1)S(1)}, bf16[3,128,256]{2,1,0:T(8,128)(2,1)S(1)}, u32[]{:S(2)}, u32[]{:S(2)}) collective-permute-start(bf16[3,128,256]{2,1,0:T(8,128)(2,1)S(1)} %get-tuple-element.98), channel_id=1, source_target_pairs={{0,7},{1,6},{2,5},{3,4},{4,3},{5,2},{6,1},{7,0},{8,15},{9,14},{10,... | collective-permute-start | bytes 589832 | tf_op jit(solution)/shard_map/ppermute | solution.py:138
  422.2 4.1 collective-permute-start.16
  426.4 7.0 %collective-permute-done.26.refs_6_ = bf16[3,128,256]{2,1,0:T(8,128)(2,1)S(1)} collective-permute-done((bf16[3,128,256]{2,1,0:T(8,128)(2,1)S(1)}, bf16[3,128,256]{2,1,0:T(8,128)(2,1)S(1)}, u32[]{:S(2)}, u32[]{:S(2)}) %collective-permute-start.26) | collective-permute-done | bytes 196640 | tf_op jit(solution)/shard_map/ppermute | solution.py:138
  433.3 6.1 collective-permute-done.27.refs_7_
  439.6 22.2 %collective-permute-done.16.refs_3_ = bf16[16,256,128]{2,1,0:T(8,128)(2,1)S(1)} collective-permute-done((bf16[16,256,128]{2,1,0:T(8,128)(2,1)S(1)}, bf16[16,256,128]{2,1,0:T(8,128)(2,1)S(1)}, u32[]{:S(2)}, u32[]{:S(2)}) %collective-permute-start.16) | collective-permute-done | bytes 1048608 | tf_op jit(solution)/shard_map/ppermute | solution.py:138
  464.3 82.9 %collective-permute-done.17.refs_4_ = bf16[16,256,128]{2,1,0:T(8,128)(2,1)S(1)} collective-permute-done((bf16[16,256,128]{2,1,0:T(8,128)(2,1)S(1)}, bf16[16,256,128]{2,1,0:T(8,128)(2,1)S(1)}, u32[]{:S(2)}, u32[]{:S(2)}) %collective-permute-start.17) | collective-permute-done | bytes 1048608 | tf_op jit(solution)/shard_map/ppermute | solution.py:138
  547.3 3.1 collective-permute-start.3
  550.4 20.8 %collective-permute-done.18.refs_5_ = bf16[16,256,128]{2,1,0:T(8,128)(2,1)S(1)} collective-permute-done((bf16[16,256,128]{2,1,0:T(8,128)(2,1)S(1)}, bf16[16,256,128]{2,1,0:T(8,128)(2,1)S(1)}, u32[]{:S(2)}, u32[]{:S(2)}) %collective-permute-start.18) | collective-permute-done | bytes 1048608 | tf_op jit(solution)/shard_map/ppermute | solution.py:138
  571.1 3.4 collective-permute-start.4
  574.5 26.0 %collective-permute-done.19.refs_6_ = bf16[16,256,128]{2,1,0:T(8,128)(2,1)S(1)} collective-permute-done((bf16[16,256,128]{2,1,0:T(8,128)(2,1)S(1)}, bf16[16,256,128]{2,1,0:T(8,128)(2,1)S(1)}, u32[]{:S(2)}, u32[]{:S(2)}) %collective-permute-start.19) | collective-permute-done | bytes 1048608 | tf_op jit(solution)/shard_map/ppermute | solution.py:138
  600.5 24.1 %collective-permute-done.20.refs_7_ = bf16[16,256,128]{2,1,0:T(8,128)(2,1)S(1)} collective-permute-done((bf16[16,256,128]{2,1,0:T(8,128)(2,1)S(1)}, bf16[16,256,128]{2,1,0:T(8,128)(2,1)S(1)}, u32[]{:S(2)}, u32[]{:S(2)}) %collective-permute-start.20) | collective-permute-done | bytes 1048608 | tf_op jit(solution)/shard_map/ppermute | solution.py:138
  628.4 5.4 shard_map.115
  633.8 7.8 %shard_map.111 = (bf16[16,2048,128]{2,1,0:T(8,128)(2,1)}, f32[16,128]{1,0:T(8,128)S(1)}) custom-call(bf16[8,12,256,128]{3,2,1,0:T(8,128)(2,1)} %all-to-all-done.refs_0_), custom_call_target="tpu_custom_call" | custom-call | tf_op jit(solution)/shard_map/pallas_call | solution.py:123
  641.7 8.0 %shard_map.121 = (bf16[16,128,2048]{2,1,0:T(8,128)(2,1)}, f32[16,128]{1,0:T(8,128)}) custom-call(bf16[8,12,128,256]{3,2,1,0:T(8,128)(2,1)} %all-to-all-done.1.refs_0_, bf16[16,128,2048]{2,1,0:T(8,128)(2,1)} %get-tuple-element.109.refs_1_, f32[16,128]{1,0:T(8,128)S(1)} %get-tuple-element.110.refs_2_), custom_call_target="tpu_custom_call", output_to_operand_aliasing={{0}: (1, {})} | custom-call | tf_op jit(solution)/shard_map/pallas_call | solution.py:123
  (91 shorter events, 54.2 us)
Async XLA Ops:
  9.0 141.0 %all-to-all-start = ((bf16[8,12,256,128]{3,2,1,0:T(8,128)(2,1)}), bf16[8,12,256,128]{3,2,1,0:T(8,128)(2,1)}, u32[]{:S(2)}, u32[]{:S(2)}) async-start(bf16[8,12,256,128]{3,2,1,0:T(8,128)(2,1)} %copy-done.1), calls=%async_computation | async-start | bytes 12582912 | tf_op jit(solution)/shard_map/all_to_all | solution.py:214
  150.0 491.6 %all-to-all-start.1 = ((bf16[8,12,128,256]{3,2,1,0:T(8,128)(2,1)}), bf16[8,12,128,256]{3,2,1,0:T(8,128)(2,1)}, u32[]{:S(2)}, u32[]{:S(2)}) async-start(bf16[8,12,128,256]{3,2,1,0:T(8,128)(2,1)} %copy-done), calls=%async_computation.1 | async-start | bytes 12582912 | tf_op jit(solution)/shard_map/all_to_all | solution.py:214
  158.3 137.1 %collective-permute-start.37 = (bf16[16,256]{1,0:T(8,128)(2,1)S(1)}, bf16[16,256]{1,0:T(8,128)(2,1)S(1)}, u32[]{:S(2)}, u32[]{:S(2)}) collective-permute-start(bf16[16,256]{1,0:T(8,128)(2,1)S(1)} %shard_map.122.refs_0_), channel_id=1, source_target_pairs={{0,6},{1,7},{2,4},{3,5},{4,2},{5,3},{6,0},{7,1},{8,14},{9,15},{10,... | collective-permute-start | bytes 24584 | tf_op jit(solution)/shard_map/ppermute | solution.py:138
  159.6 135.9 %collective-permute-start.36 = (bf16[16,256]{1,0:T(8,128)(2,1)S(1)}, bf16[16,256]{1,0:T(8,128)(2,1)S(1)}, u32[]{:S(2)}, u32[]{:S(2)}) collective-permute-start(bf16[16,256]{1,0:T(8,128)(2,1)S(1)} %shard_map.122.refs_0_), channel_id=1, source_target_pairs={{0,4},{1,5},{2,6},{3,7},{4,0},{5,1},{6,2},{7,3},{8,12},{9,13},{10,... | collective-permute-start | bytes 24584 | tf_op jit(solution)/shard_map/ppermute | solution.py:138
  160.6 134.9 %collective-permute-start.35 = (bf16[16,256]{1,0:T(8,128)(2,1)S(1)}, bf16[16,256]{1,0:T(8,128)(2,1)S(1)}, u32[]{:S(2)}, u32[]{:S(2)}) collective-permute-start(bf16[16,256]{1,0:T(8,128)(2,1)S(1)} %shard_map.122.refs_0_), channel_id=1, source_target_pairs={{0,2},{1,3},{2,0},{3,1},{4,6},{5,7},{6,4},{7,5},{8,10},{9,11},{10,... | collective-permute-start | bytes 24584 | tf_op jit(solution)/shard_map/ppermute | solution.py:138
  304.3 13.2 %collective-permute-start.28 = (bf16[1,128,256]{2,1,0:T(8,128)(2,1)S(1)}, bf16[1,128,256]{2,1,0:T(8,128)(2,1)S(1)}, u32[]{:S(2)}, u32[]{:S(2)}) collective-permute-start(bf16[1,128,256]{2,1,0:T(8,128)(2,1)S(1)} %get-tuple-element.100), channel_id=1, source_target_pairs={{0,1},{1,0},{2,3},{3,2},{4,5},{5,4},{6,7},{7,6},{8,9},{9,8},{10,11... | collective-permute-start | bytes 196616 | tf_op jit(solution)/shard_map/ppermute | solution.py:138
  305.1 12.6 %collective-permute-start.29 = (bf16[1,128,256]{2,1,0:T(8,128)(2,1)S(1)}, bf16[1,128,256]{2,1,0:T(8,128)(2,1)S(1)}, u32[]{:S(2)}, u32[]{:S(2)}) collective-permute-start(bf16[1,128,256]{2,1,0:T(8,128)(2,1)S(1)} %get-tuple-element.101), channel_id=1, source_target_pairs={{0,2},{1,3},{2,0},{3,1},{4,6},{5,7},{6,4},{7,5},{8,10},{9,11},{10,... | collective-permute-start | bytes 196616 | tf_op jit(solution)/shard_map/ppermute | solution.py:138
  306.8 13.5 %collective-permute-start.31 = (bf16[1,128,256]{2,1,0:T(8,128)(2,1)S(1)}, bf16[1,128,256]{2,1,0:T(8,128)(2,1)S(1)}, u32[]{:S(2)}, u32[]{:S(2)}) collective-permute-start(bf16[1,128,256]{2,1,0:T(8,128)(2,1)S(1)} %get-tuple-element.103), channel_id=1, source_target_pairs={{0,4},{1,5},{2,6},{3,7},{4,0},{5,1},{6,2},{7,3},{8,12},{9,13},{10,... | collective-permute-start | bytes 196616 | tf_op jit(solution)/shard_map/ppermute | solution.py:138
  306.9 14.5 %collective-permute-start.32 = (bf16[1,128,256]{2,1,0:T(8,128)(2,1)S(1)}, bf16[1,128,256]{2,1,0:T(8,128)(2,1)S(1)}, u32[]{:S(2)}, u32[]{:S(2)}) collective-permute-start(bf16[1,128,256]{2,1,0:T(8,128)(2,1)S(1)} %get-tuple-element.104), channel_id=1, source_target_pairs={{0,5},{1,4},{2,7},{3,6},{4,1},{5,0},{6,3},{7,2},{8,13},{9,12},{10,... | collective-permute-start | bytes 196616 | tf_op jit(solution)/shard_map/ppermute | solution.py:138
  317.6 121.8 %collective-permute-start.14 = (bf16[16,256,128]{2,1,0:T(8,128)(2,1)S(1)}, bf16[16,256,128]{2,1,0:T(8,128)(2,1)S(1)}, u32[]{:S(2)}, u32[]{:S(2)}) collective-permute-start(bf16[16,256,128]{2,1,0:T(8,128)(2,1)S(1)} %get-tuple-element.83), channel_id=1, source_target_pairs={{0,1},{1,0},{2,3},{3,2},{4,5},{5,4},{6,7},{7,6},{8,9},{9,8},{10,11... | collective-permute-start | bytes 3145736 | tf_op jit(solution)/shard_map/ppermute | solution.py:138
  317.7 121.8 %collective-permute-start.15 = (bf16[16,256,128]{2,1,0:T(8,128)(2,1)S(1)}, bf16[16,256,128]{2,1,0:T(8,128)(2,1)S(1)}, u32[]{:S(2)}, u32[]{:S(2)}) collective-permute-start(bf16[16,256,128]{2,1,0:T(8,128)(2,1)S(1)} %get-tuple-element.84), channel_id=1, source_target_pairs={{0,2},{1,3},{2,0},{3,1},{4,6},{5,7},{6,4},{7,5},{8,10},{9,11},{10,... | collective-permute-start | bytes 3145736 | tf_op jit(solution)/shard_map/ppermute | solution.py:138
  320.4 44.2 %collective-permute-start.7 = (bf16[3,256,128]{2,1,0:T(8,128)(2,1)S(1)}, bf16[3,256,128]{2,1,0:T(8,128)(2,1)S(1)}, u32[]{:S(2)}, u32[]{:S(2)}) collective-permute-start(bf16[3,256,128]{2,1,0:T(8,128)(2,1)S(1)} %get-tuple-element.70), channel_id=1, source_target_pairs={{0,1},{1,0},{2,3},{3,2},{4,5},{5,4},{6,7},{7,6},{8,9},{9,8},{10,11... | collective-permute-start | bytes 589832 | tf_op jit(solution)/shard_map/ppermute | solution.py:138
  321.4 43.2 %collective-permute-start.8 = (bf16[3,256,128]{2,1,0:T(8,128)(2,1)S(1)}, bf16[3,256,128]{2,1,0:T(8,128)(2,1)S(1)}, u32[]{:S(2)}, u32[]{:S(2)}) collective-permute-start(bf16[3,256,128]{2,1,0:T(8,128)(2,1)S(1)} %get-tuple-element.71), channel_id=1, source_target_pairs={{0,2},{1,3},{2,0},{3,1},{4,6},{5,7},{6,4},{7,5},{8,10},{9,11},{10,... | collective-permute-start | bytes 589832 | tf_op jit(solution)/shard_map/ppermute | solution.py:138
  337.7 31.3 %collective-permute-start.9 = (bf16[3,256,128]{2,1,0:T(8,128)(2,1)S(1)}, bf16[3,256,128]{2,1,0:T(8,128)(2,1)S(1)}, u32[]{:S(2)}, u32[]{:S(2)}) collective-permute-start(bf16[3,256,128]{2,1,0:T(8,128)(2,1)S(1)} %get-tuple-element.72), channel_id=1, source_target_pairs={{0,3},{1,2},{2,1},{3,0},{4,7},{5,6},{6,5},{7,4},{8,11},{9,10},{10,... | collective-permute-start | bytes 589832 | tf_op jit(solution)/shard_map/ppermute | solution.py:138
  364.6 15.6 %collective-permute-start.10 = (bf16[3,256,128]{2,1,0:T(8,128)(2,1)S(1)}, bf16[3,256,128]{2,1,0:T(8,128)(2,1)S(1)}, u32[]{:S(2)}, u32[]{:S(2)}) collective-permute-start(bf16[3,256,128]{2,1,0:T(8,128)(2,1)S(1)} %get-tuple-element.73), channel_id=1, source_target_pairs={{0,4},{1,5},{2,6},{3,7},{4,0},{5,1},{6,2},{7,3},{8,12},{9,13},{10,... | collective-permute-start | bytes 589832 | tf_op jit(solution)/shard_map/ppermute | solution.py:138
  364.6 19.9 %collective-permute-start.11 = (bf16[3,256,128]{2,1,0:T(8,128)(2,1)S(1)}, bf16[3,256,128]{2,1,0:T(8,128)(2,1)S(1)}, u32[]{:S(2)}, u32[]{:S(2)}) collective-permute-start(bf16[3,256,128]{2,1,0:T(8,128)(2,1)S(1)} %get-tuple-element.74), channel_id=1, source_target_pairs={{0,5},{1,4},{2,7},{3,6},{4,1},{5,0},{6,3},{7,2},{8,13},{9,12},{10,... | collective-permute-start | bytes 589832 | tf_op jit(solution)/shard_map/ppermute | solution.py:138
  369.0 27.4 %collective-permute-start.12 = (bf16[3,256,128]{2,1,0:T(8,128)(2,1)S(1)}, bf16[3,256,128]{2,1,0:T(8,128)(2,1)S(1)}, u32[]{:S(2)}, u32[]{:S(2)}) collective-permute-start(bf16[3,256,128]{2,1,0:T(8,128)(2,1)S(1)} %get-tuple-element.75), channel_id=1, source_target_pairs={{0,6},{1,7},{2,4},{3,5},{4,2},{5,3},{6,0},{7,1},{8,14},{9,15},{10,... | collective-permute-start | bytes 589832 | tf_op jit(solution)/shard_map/ppermute | solution.py:138
  380.2 20.8 %collective-permute-start.13 = (bf16[3,256,128]{2,1,0:T(8,128)(2,1)S(1)}, bf16[3,256,128]{2,1,0:T(8,128)(2,1)S(1)}, u32[]{:S(2)}, u32[]{:S(2)}) collective-permute-start(bf16[3,256,128]{2,1,0:T(8,128)(2,1)S(1)} %get-tuple-element.76), channel_id=1, source_target_pairs={{0,7},{1,6},{2,5},{3,4},{4,3},{5,2},{6,1},{7,0},{8,15},{9,14},{10,... | collective-permute-start | bytes 589832 | tf_op jit(solution)/shard_map/ppermute | solution.py:138
  384.5 16.4 %collective-permute-start.21 = (bf16[3,128,256]{2,1,0:T(8,128)(2,1)S(1)}, bf16[3,128,256]{2,1,0:T(8,128)(2,1)S(1)}, u32[]{:S(2)}, u32[]{:S(2)}) collective-permute-start(bf16[3,128,256]{2,1,0:T(8,128)(2,1)S(1)} %get-tuple-element.92), channel_id=1, source_target_pairs={{0,1},{1,0},{2,3},{3,2},{4,5},{5,4},{6,7},{7,6},{8,9},{9,8},{10,11... | collective-permute-start | bytes 589832 | tf_op jit(solution)/shard_map/ppermute | solution.py:138
  401.7 20.5 %collective-permute-start.25 = (bf16[3,128,256]{2,1,0:T(8,128)(2,1)S(1)}, bf16[3,128,256]{2,1,0:T(8,128)(2,1)S(1)}, u32[]{:S(2)}, u32[]{:S(2)}) collective-permute-start(bf16[3,128,256]{2,1,0:T(8,128)(2,1)S(1)} %get-tuple-element.96), channel_id=1, source_target_pairs={{0,5},{1,4},{2,7},{3,6},{4,1},{5,0},{6,3},{7,2},{8,13},{9,12},{10,... | collective-permute-start | bytes 589832 | tf_op jit(solution)/shard_map/ppermute | solution.py:138
  408.7 24.6 %collective-permute-start.26 = (bf16[3,128,256]{2,1,0:T(8,128)(2,1)S(1)}, bf16[3,128,256]{2,1,0:T(8,128)(2,1)S(1)}, u32[]{:S(2)}, u32[]{:S(2)}) collective-permute-start(bf16[3,128,256]{2,1,0:T(8,128)(2,1)S(1)} %get-tuple-element.97), channel_id=1, source_target_pairs={{0,6},{1,7},{2,4},{3,5},{4,2},{5,3},{6,0},{7,1},{8,14},{9,15},{10,... | collective-permute-start | bytes 589832 | tf_op jit(solution)/shard_map/ppermute | solution.py:138
  411.4 28.1 %collective-permute-start.27 = (bf16[3,128,256]{2,1,0:T(8,128)(2,1)S(1)}, bf16[3,128,256]{2,1,0:T(8,128)(2,1)S(1)}, u32[]{:S(2)}, u32[]{:S(2)}) collective-permute-start(bf16[3,128,256]{2,1,0:T(8,128)(2,1)S(1)} %get-tuple-element.98), channel_id=1, source_target_pairs={{0,7},{1,6},{2,5},{3,4},{4,3},{5,2},{6,1},{7,0},{8,15},{9,14},{10,... | collective-permute-start | bytes 589832 | tf_op jit(solution)/shard_map/ppermute | solution.py:138
  422.2 39.6 %collective-permute-start.16 = (bf16[16,256,128]{2,1,0:T(8,128)(2,1)S(1)}, bf16[16,256,128]{2,1,0:T(8,128)(2,1)S(1)}, u32[]{:S(2)}, u32[]{:S(2)}) collective-permute-start(bf16[16,256,128]{2,1,0:T(8,128)(2,1)S(1)} %get-tuple-element.85), channel_id=1, source_target_pairs={{0,3},{1,2},{2,1},{3,0},{4,7},{5,6},{6,5},{7,4},{8,11},{9,10},{10,... | collective-permute-start | bytes 3145736 | tf_op jit(solution)/shard_map/ppermute | solution.py:138
  433.3 113.9 %collective-permute-start.17 = (bf16[16,256,128]{2,1,0:T(8,128)(2,1)S(1)}, bf16[16,256,128]{2,1,0:T(8,128)(2,1)S(1)}, u32[]{:S(2)}, u32[]{:S(2)}) collective-permute-start(bf16[16,256,128]{2,1,0:T(8,128)(2,1)S(1)} %get-tuple-element.86), channel_id=1, source_target_pairs={{0,4},{1,5},{2,6},{3,7},{4,0},{5,1},{6,2},{7,3},{8,12},{9,13},{10,... | collective-permute-start | bytes 3145736 | tf_op jit(solution)/shard_map/ppermute | solution.py:138
  439.4 131.7 %collective-permute-start.18 = (bf16[16,256,128]{2,1,0:T(8,128)(2,1)S(1)}, bf16[16,256,128]{2,1,0:T(8,128)(2,1)S(1)}, u32[]{:S(2)}, u32[]{:S(2)}) collective-permute-start(bf16[16,256,128]{2,1,0:T(8,128)(2,1)S(1)} %get-tuple-element.87), channel_id=1, source_target_pairs={{0,5},{1,4},{2,7},{3,6},{4,1},{5,0},{6,3},{7,2},{8,13},{9,12},{10,... | collective-permute-start | bytes 3145736 | tf_op jit(solution)/shard_map/ppermute | solution.py:138
  439.4 161.0 %collective-permute-start.19 = (bf16[16,256,128]{2,1,0:T(8,128)(2,1)S(1)}, bf16[16,256,128]{2,1,0:T(8,128)(2,1)S(1)}, u32[]{:S(2)}, u32[]{:S(2)}) collective-permute-start(bf16[16,256,128]{2,1,0:T(8,128)(2,1)S(1)} %copy-done.5), channel_id=1, source_target_pairs={{0,6},{1,7},{2,4},{3,5},{4,2},{5,3},{6,0},{7,1},{8,14},{9,15},{10,... | collective-permute-start | bytes 3145736 | tf_op jit(solution)/shard_map/ppermute | solution.py:138
  439.5 185.0 %collective-permute-start.20 = (bf16[16,256,128]{2,1,0:T(8,128)(2,1)S(1)}, bf16[16,256,128]{2,1,0:T(8,128)(2,1)S(1)}, u32[]{:S(2)}, u32[]{:S(2)}) collective-permute-start(bf16[16,256,128]{2,1,0:T(8,128)(2,1)S(1)} %copy-done.4), channel_id=1, source_target_pairs={{0,7},{1,6},{2,5},{3,4},{4,3},{5,2},{6,1},{7,0},{8,15},{9,14},{10,... | collective-permute-start | bytes 3145736 | tf_op jit(solution)/shard_map/ppermute | solution.py:138
  461.8 189.6 %collective-permute-start.2 = (bf16[1,256,128]{2,1,0:T(8,128)(2,1)S(1)}, bf16[1,256,128]{2,1,0:T(8,128)(2,1)S(1)}, u32[]{:S(2)}, u32[]{:S(2)}) collective-permute-start(bf16[1,256,128]{2,1,0:T(8,128)(2,1)S(1)} %get-tuple-element.64), channel_id=1, source_target_pairs={{0,3},{1,2},{2,1},{3,0},{4,7},{5,6},{6,5},{7,4},{8,11},{9,10},{10,... | collective-permute-start | bytes 196616 | tf_op jit(solution)/shard_map/ppermute | solution.py:138
  547.3 104.2 %collective-permute-start.3 = (bf16[1,256,128]{2,1,0:T(8,128)(2,1)S(1)}, bf16[1,256,128]{2,1,0:T(8,128)(2,1)S(1)}, u32[]{:S(2)}, u32[]{:S(2)}) collective-permute-start(bf16[1,256,128]{2,1,0:T(8,128)(2,1)S(1)} %get-tuple-element.65), channel_id=1, source_target_pairs={{0,4},{1,5},{2,6},{3,7},{4,0},{5,1},{6,2},{7,3},{8,12},{9,13},{10,... | collective-permute-start | bytes 196616 | tf_op jit(solution)/shard_map/ppermute | solution.py:138
  571.1 80.4 %collective-permute-start.4 = (bf16[1,256,128]{2,1,0:T(8,128)(2,1)S(1)}, bf16[1,256,128]{2,1,0:T(8,128)(2,1)S(1)}, u32[]{:S(2)}, u32[]{:S(2)}) collective-permute-start(bf16[1,256,128]{2,1,0:T(8,128)(2,1)S(1)} %get-tuple-element.66), channel_id=1, source_target_pairs={{0,5},{1,4},{2,7},{3,6},{4,1},{5,0},{6,3},{7,2},{8,13},{9,12},{10,... | collective-permute-start | bytes 196616 | tf_op jit(solution)/shard_map/ppermute | solution.py:138
  600.5 51.0 %collective-permute-start.5 = (bf16[1,256,128]{2,1,0:T(8,128)(2,1)S(1)}, bf16[1,256,128]{2,1,0:T(8,128)(2,1)S(1)}, u32[]{:S(2)}, u32[]{:S(2)}) collective-permute-start(bf16[1,256,128]{2,1,0:T(8,128)(2,1)S(1)} %get-tuple-element.67), channel_id=1, source_target_pairs={{0,6},{1,7},{2,4},{3,5},{4,2},{5,3},{6,0},{7,1},{8,14},{9,15},{10,... | collective-permute-start | bytes 196616 | tf_op jit(solution)/shard_map/ppermute | solution.py:138
  624.6 26.9 %collective-permute-start.6 = (bf16[1,256,128]{2,1,0:T(8,128)(2,1)S(1)}, bf16[1,256,128]{2,1,0:T(8,128)(2,1)S(1)}, u32[]{:S(2)}, u32[]{:S(2)}) collective-permute-start(bf16[1,256,128]{2,1,0:T(8,128)(2,1)S(1)} %get-tuple-element.68), channel_id=1, source_target_pairs={{0,7},{1,6},{2,5},{3,4},{4,3},{5,2},{6,1},{7,0},{8,15},{9,14},{10,... | collective-permute-start | bytes 196616 | tf_op jit(solution)/shard_map/ppermute | solution.py:138
  (21 other events, 520.2 us)
where the time goes:
time: 653 us
  waiting for transfers between devices  484 us (74%)
  starting transfers between devices  109 us (17%)
  Pallas kernels  54 us (8%)
    ppermute x45, waiting for transfers between devices, exchange(): return lax.ppermute(x, name, [(i, i ^ k) for i in range(size)])  356 us
    all_to_all x2, waiting for transfers between devices, by_pieces(): pieces = lax.all_to_all(pieces, 'zero', 0, 0, tiled=True)  128 us
    ppermute x45, starting transfers between devices, exchange(): return lax.ppermute(x, name, [(i, i ^ k) for i in range(size)])  95 us
    pallas_call x7, Pallas kernels, serve(): pl.pallas_call(functools.partial(serve_kernel, axis, first, single, n, he...  27.2 us
    pallas_call x7, Pallas kernels, narrow(): pl.pallas_call(kernel, grid=(count // size,), in_specs=[pl.BlockSpec((siz...  26 us
    all_to_all x2, starting transfers between devices, by_pieces(): pieces = lax.all_to_all(pieces, 'zero', 0, 0, tiled=True)  13.8 us
  transfers between devices with their start and end apart: 47, of which 21 were waited for; matrix products, arithmetic and copies ran while one was open for 0% of the time, Pallas kernels for 7%

commit v1 on v0

--- a/solution.py
+++ b/solution.py
@@ -57,6 +57,40 @@
         compiler_params=pltpu.CompilerParams(
             dimension_semantics=("arbitrary",), vmem_limit_bytes=LARGE
         ),
+    )(x)
+
+
+def narrow_some_kernel(axis, first, places, x_ref, *refs):
+    out_refs, (wide_ref, sems) = refs[: len(places)], refs[len(places) :]
+    me = lax.axis_index("zero")
+    copies = []
+    for slot, k in enumerate(places):
+        count, *shape = wide_ref.shape[1:]
+        size = shape[axis - 1]
+        at = pl.ds(pl.multiple_of((me ^ k) * size, size), size)
+        window = (at, slice(None)) if axis == 1 else (slice(None), at)
+        source = x_ref.at[(pl.ds(first, count), *window)]
+        copies.append(pltpu.make_async_copy(source, wide_ref.at[slot], sems.at[slot]))
+        copies[-1].start()
+    for slot, out_ref in enumerate(out_refs):
+        copies[slot].wait()
+        out_ref[...] = wide_ref[slot].astype(jnp.bfloat16)
+
+
+def narrow_some(x, axis, first, count, n, places):
+    shape = list(x.shape[1:])
+    shape[axis - 1] //= n
+    out = jax.ShapeDtypeStruct((count, *shape), jnp.bfloat16)
+    return pl.pallas_call(
+        functools.partial(narrow_some_kernel, axis, first, places),
+        in_specs=[pl.BlockSpec(memory_space=pl.ANY)],
+        out_specs=[pl.BlockSpec(memory_space=pltpu.VMEM)] * len(places),
+        out_shape=[out] * len(places),
+        scratch_shapes=[
+            pltpu.VMEM((len(places), count, *shape), jnp.float32),
+            pltpu.SemaphoreType.DMA((len(places),)),
+        ],
+        compiler_params=pltpu.CompilerParams(vmem_limit_bytes=LARGE),
     )(x)
 
 
@@ -208,8 +242,14 @@
     axes = (2, 2, 1)
     experts = masters[0].shape[0]
     arrived = []
-    for tensor, first, count, single in chunks(experts):
-        pieces = narrow(masters[tensor], axes[tensor], first, count, n, single)
+    for c, (tensor, first, count, single) in enumerate(chunks(experts)):
+        if c == 0:
+            near, far = list(range(n // 2)), list(range(n // 2, n))
+            pieces = narrow_some(masters[tensor], axes[tensor], first, count, n, far)
+            others = narrow_some(masters[tensor], axes[tensor], first, count, n, near)
+            pieces = [*others, *pieces]
+        else:
+            pieces = narrow(masters[tensor], axes[tensor], first, count, n, single)
         if single:
             pieces = lax.all_to_all(pieces, "zero", 0, 0, tiled=True)
         else:

time: 653 us -> 656 us (level)
  the two profiles are of different devices: /device:TPU:9 before, /device:TPU:17 now
where the time goes in v1:
time: 656 us
  waiting for transfers between devices  524 us (80%)
  starting transfers between devices  70.8 us (11%)
  Pallas kernels  55.1 us (8%)
    ppermute x45, waiting for transfers between devices, exchange(): return lax.ppermute(x, name, [(i, i ^ k) for i in range(size)])  397 us
    all_to_all x2, waiting for transfers between devices, by_pieces(): pieces = lax.all_to_all(pieces, 'zero', 0, 0, tiled=True)  127 us
    ppermute x45, starting transfers between devices, exchange(): return lax.ppermute(x, name, [(i, i ^ k) for i in range(size)])  56.7 us
    pallas_call x7, Pallas kernels, serve(): pl.pallas_call(functools.partial(serve_kernel, axis, first, single, n, he...  27.2 us
    pallas_call x6, Pallas kernels, narrow(): pl.pallas_call(kernel, grid=(count // size,), in_specs=[pl.BlockSpec((siz...  24.9 us
    all_to_all x2, starting transfers between devices, by_pieces(): pieces = lax.all_to_all(pieces, 'zero', 0, 0, tiled=True)  14.1 us
  transfers between devices with their start and end apart: 47, of which 23 were waited for; matrix products, arithmetic and copies ran while one was open for 0% of the time, Pallas kernels for 7%

profile of v1, /device:TPU:17, one launch (start us, length us, event | category | flops | bytes accessed | tf_op | source)
XLA Modules:
  0.0 655.7 jit_solution(4549584512248668774)
XLA Ops:
  0.6 5.7 shard_map.110
  9.0 5.5 all-to-all-start
  14.5 5.3 shard_map.116
  22.4 127.2 %all-to-all-done.refs_0_ = bf16[8,12,256,128]{3,2,1,0:T(8,128)(2,1)} async-done(((bf16[8,12,256,128]{3,2,1,0:T(8,128)(2,1)}), bf16[8,12,256,128]{3,2,1,0:T(8,128)(2,1)}, u32[]{:S(2)}, u32[]{:S(2)}) %all-to-all-start) | async-done | bytes 6291488 | tf_op jit(solution)/shard_map/all_to_all | solution.py:254
  149.6 8.6 %all-to-all-start.1 = ((bf16[8,12,128,256]{3,2,1,0:T(8,128)(2,1)}), bf16[8,12,128,256]{3,2,1,0:T(8,128)(2,1)}, u32[]{:S(2)}, u32[]{:S(2)}) async-start(bf16[8,12,128,256]{3,2,1,0:T(8,128)(2,1)} %copy-done), calls=%async_computation.1 | async-start | bytes 12582912 | tf_op jit(solution)/shard_map/all_to_all | solution.py:254
  158.5 3.0 collective-permute-start.36
  161.5 133.5 %collective-permute-done.37.refs_3_ = bf16[16,256]{1,0:T(8,128)(2,1)S(1)} collective-permute-done((bf16[16,256]{1,0:T(8,128)(2,1)S(1)}, bf16[16,256]{1,0:T(8,128)(2,1)S(1)}, u32[]{:S(2)}, u32[]{:S(2)}) %collective-permute-start.37) | collective-permute-done | bytes 8224 | tf_op jit(solution)/shard_map/ppermute | solution.py:172
  306.0 4.0 collective-permute-done.31.refs_4_
  313.8 8.1 %shard_map.114 = (bf16[16,256,128]{2,1,0:T(8,128)(2,1)S(1)}, bf16[16,256,128]{2,1,0:T(8,128)(2,1)S(1)}, bf16[16,256,128]{2,1,0:T(8,128)(2,1)S(1)}, bf16[16,256,1...) custom-call(f32[16,256,1024]{2,1,0:T(8,128)} %x_ref.11), custom_call_target="tpu_custom_call" | custom-call | tf_op jit(solution)/shard_map/pallas_call | solution.py:51
  328.1 23.8 %collective-permute-done.1.refs_2_ = bf16[1,256,128]{2,1,0:T(8,128)(2,1)S(1)} collective-permute-done((bf16[1,256,128]{2,1,0:T(8,128)(2,1)S(1)}, bf16[1,256,128]{2,1,0:T(8,128)(2,1)S(1)}, u32[]{:S(2)}, u32[]{:S(2)}) %collective-permute-start.1) | collective-permute-done | bytes 65568 | tf_op jit(solution)/shard_map/ppermute | solution.py:172
  361.4 4.3 collective-permute-start.9
  370.5 3.9 collective-permute-done.9.refs_3_
  374.4 11.2 %collective-permute-done.10.refs_4_ = bf16[3,256,128]{2,1,0:T(8,128)(2,1)S(1)} collective-permute-done((bf16[3,256,128]{2,1,0:T(8,128)(2,1)S(1)}, bf16[3,256,128]{2,1,0:T(8,128)(2,1)S(1)}, u32[]{:S(2)}, u32[]{:S(2)}) %collective-permute-start.10) | collective-permute-done | bytes 196640 | tf_op jit(solution)/shard_map/ppermute | solution.py:172
  385.6 4.1 collective-permute-done.11.refs_5_
  389.7 9.1 %collective-permute-done.12.refs_6_ = bf16[3,256,128]{2,1,0:T(8,128)(2,1)S(1)} collective-permute-done((bf16[3,256,128]{2,1,0:T(8,128)(2,1)S(1)}, bf16[3,256,128]{2,1,0:T(8,128)(2,1)S(1)}, u32[]{:S(2)}, u32[]{:S(2)}) %collective-permute-start.12) | collective-permute-done | bytes 196640 | tf_op jit(solution)/shard_map/ppermute | solution.py:172
  398.8 3.2 collective-permute-done.13.refs_7_
  402.0 3.7 collective-permute-start.24
  411.2 11.8 %collective-permute-done.24.refs_4_ = bf16[3,128,256]{2,1,0:T(8,128)(2,1)S(1)} collective-permute-done((bf16[3,128,256]{2,1,0:T(8,128)(2,1)S(1)}, bf16[3,128,256]{2,1,0:T(8,128)(2,1)S(1)}, u32[]{:S(2)}, u32[]{:S(2)}) %collective-permute-start.24) | collective-permute-done | bytes 196640 | tf_op jit(solution)/shard_map/ppermute | solution.py:172
  423.0 4.2 collective-permute-done.25.refs_5_
  427.2 6.0 collective-permute-start.16
  433.2 2.8 collective-permute-done.26.refs_6_
  436.0 4.5 collective-permute-done.27.refs_7_
  442.5 27.7 %collective-permute-done.16.refs_3_ = bf16[16,256,128]{2,1,0:T(8,128)(2,1)S(1)} collective-permute-done((bf16[16,256,128]{2,1,0:T(8,128)(2,1)S(1)}, bf16[16,256,128]{2,1,0:T(8,128)(2,1)S(1)}, u32[]{:S(2)}, u32[]{:S(2)}) %collective-permute-start.16) | collective-permute-done | bytes 1048608 | tf_op jit(solution)/shard_map/ppermute | solution.py:172
  472.7 79.6 %collective-permute-done.17.refs_4_ = bf16[16,256,128]{2,1,0:T(8,128)(2,1)S(1)} collective-permute-done((bf16[16,256,128]{2,1,0:T(8,128)(2,1)S(1)}, bf16[16,256,128]{2,1,0:T(8,128)(2,1)S(1)}, u32[]{:S(2)}, u32[]{:S(2)}) %collective-permute-start.17) | collective-permute-done | bytes 1048608 | tf_op jit(solution)/shard_map/ppermute | solution.py:172
  552.2 3.1 collective-permute-start.3
  555.3 20.8 %collective-permute-done.18.refs_5_ = bf16[16,256,128]{2,1,0:T(8,128)(2,1)S(1)} collective-permute-done((bf16[16,256,128]{2,1,0:T(8,128)(2,1)S(1)}, bf16[16,256,128]{2,1,0:T(8,128)(2,1)S(1)}, u32[]{:S(2)}, u32[]{:S(2)}) %collective-permute-start.18) | collective-permute-done | bytes 1048608 | tf_op jit(solution)/shard_map/ppermute | solution.py:172
  576.1 3.4 collective-permute-start.4
  579.5 23.7 %collective-permute-done.19.refs_6_ = bf16[16,256,128]{2,1,0:T(8,128)(2,1)S(1)} collective-permute-done((bf16[16,256,128]{2,1,0:T(8,128)(2,1)S(1)}, bf16[16,256,128]{2,1,0:T(8,128)(2,1)S(1)}, u32[]{:S(2)}, u32[]{:S(2)}) %collective-permute-start.19) | collective-permute-done | bytes 1048608 | tf_op jit(solution)/shard_map/ppermute | solution.py:172
  605.0 20.6 %collective-permute-done.20.refs_7_ = bf16[16,256,128]{2,1,0:T(8,128)(2,1)S(1)} collective-permute-done((bf16[16,256,128]{2,1,0:T(8,128)(2,1)S(1)}, bf16[16,256,128]{2,1,0:T(8,128)(2,1)S(1)}, u32[]{:S(2)}, u32[]{:S(2)}) %collective-permute-start.20) | collective-permute-done | bytes 1048608 | tf_op jit(solution)/shard_map/ppermute | solution.py:172
  631.6 5.4 shard_map.115
  637.0 7.8 %shard_map.111 = (bf16[16,2048,128]{2,1,0:T(8,128)(2,1)}, f32[16,128]{1,0:T(8,128)S(1)}) custom-call(bf16[8,12,256,128]{3,2,1,0:T(8,128)(2,1)} %all-to-all-done.refs_0_), custom_call_target="tpu_custom_call" | custom-call | tf_op jit(solution)/shard_map/pallas_call | solution.py:157
  644.8 8.0 %shard_map.122 = (bf16[16,128,2048]{2,1,0:T(8,128)(2,1)}, f32[16,128]{1,0:T(8,128)}) custom-call(bf16[8,12,128,256]{3,2,1,0:T(8,128)(2,1)} %all-to-all-done.1.refs_0_, bf16[16,128,2048]{2,1,0:T(8,128)(2,1)} %get-tuple-element.109.refs_1_, f32[16,128]{1,0:T(8,128)S(1)} %get-tuple-element.110.refs_2_), custom_call_target="tpu_custom_call", output_to_operand_aliasing={{0}: (1, {})} | custom-call | tf_op jit(solution)/shard_map/pallas_call | solution.py:157
  (92 shorter events, 61.7 us)
Async XLA Ops:
  9.0 140.6 %all-to-all-start = ((bf16[8,12,256,128]{3,2,1,0:T(8,128)(2,1)}), bf16[8,12,256,128]{3,2,1,0:T(8,128)(2,1)}, u32[]{:S(2)}, u32[]{:S(2)}) async-start(bf16[8,12,256,128]{3,2,1,0:T(8,128)(2,1)} %copy-done.1), calls=%async_computation | async-start | bytes 12582912 | tf_op jit(solution)/shard_map/all_to_all | solution.py:254
  149.6 495.3 %all-to-all-start.1 = ((bf16[8,12,128,256]{3,2,1,0:T(8,128)(2,1)}), bf16[8,12,128,256]{3,2,1,0:T(8,128)(2,1)}, u32[]{:S(2)}, u32[]{:S(2)}) async-start(bf16[8,12,128,256]{3,2,1,0:T(8,128)(2,1)} %copy-done), calls=%async_computation.1 | async-start | bytes 12582912 | tf_op jit(solution)/shard_map/all_to_all | solution.py:254
  158.2 136.8 %collective-permute-start.37 = (bf16[16,256]{1,0:T(8,128)(2,1)S(1)}, bf16[16,256]{1,0:T(8,128)(2,1)S(1)}, u32[]{:S(2)}, u32[]{:S(2)}) collective-permute-start(bf16[16,256]{1,0:T(8,128)(2,1)S(1)} %shard_map.123.refs_0_), channel_id=1, source_target_pairs={{0,6},{1,7},{2,4},{3,5},{4,2},{5,3},{6,0},{7,1},{8,14},{9,15},{10,... | collective-permute-start | bytes 24584 | tf_op jit(solution)/shard_map/ppermute | solution.py:172
  158.5 136.5 %collective-permute-start.36 = (bf16[16,256]{1,0:T(8,128)(2,1)S(1)}, bf16[16,256]{1,0:T(8,128)(2,1)S(1)}, u32[]{:S(2)}, u32[]{:S(2)}) collective-permute-start(bf16[16,256]{1,0:T(8,128)(2,1)S(1)} %shard_map.123.refs_0_), channel_id=1, source_target_pairs={{0,4},{1,5},{2,6},{3,7},{4,0},{5,1},{6,2},{7,3},{8,12},{9,13},{10,... | collective-permute-start | bytes 24584 | tf_op jit(solution)/shard_map/ppermute | solution.py:172
  161.5 133.5 %collective-permute-start.35 = (bf16[16,256]{1,0:T(8,128)(2,1)S(1)}, bf16[16,256]{1,0:T(8,128)(2,1)S(1)}, u32[]{:S(2)}, u32[]{:S(2)}) collective-permute-start(bf16[16,256]{1,0:T(8,128)(2,1)S(1)} %shard_map.123.refs_0_), channel_id=1, source_target_pairs={{0,2},{1,3},{2,0},{3,1},{4,6},{5,7},{6,4},{7,5},{8,10},{9,11},{10,... | collective-permute-start | bytes 24584 | tf_op jit(solution)/shard_map/ppermute | solution.py:172
  302.8 19.0 %collective-permute-start.33 = (bf16[1,128,256]{2,1,0:T(8,128)(2,1)S(1)}, bf16[1,128,256]{2,1,0:T(8,128)(2,1)S(1)}, u32[]{:S(2)}, u32[]{:S(2)}) collective-permute-start(bf16[1,128,256]{2,1,0:T(8,128)(2,1)S(1)} %get-tuple-element.105), channel_id=1, source_target_pairs={{0,6},{1,7},{2,4},{3,5},{4,2},{5,3},{6,0},{7,1},{8,14},{9,15},{10,... | collective-permute-start | bytes 196616 | tf_op jit(solution)/shard_map/ppermute | solution.py:172
  304.3 17.7 %collective-permute-start.34 = (bf16[1,128,256]{2,1,0:T(8,128)(2,1)S(1)}, bf16[1,128,256]{2,1,0:T(8,128)(2,1)S(1)}, u32[]{:S(2)}, u32[]{:S(2)}) collective-permute-start(bf16[1,128,256]{2,1,0:T(8,128)(2,1)S(1)} %get-tuple-element.106), channel_id=1, source_target_pairs={{0,7},{1,6},{2,5},{3,4},{4,3},{5,2},{6,1},{7,0},{8,15},{9,14},{10,... | collective-permute-start | bytes 196616 | tf_op jit(solution)/shard_map/ppermute | solution.py:172
  305.9 17.4 %collective-permute-start.28 = (bf16[1,128,256]{2,1,0:T(8,128)(2,1)S(1)}, bf16[1,128,256]{2,1,0:T(8,128)(2,1)S(1)}, u32[]{:S(2)}, u32[]{:S(2)}) collective-permute-start(bf16[1,128,256]{2,1,0:T(8,128)(2,1)S(1)} %get-tuple-element.100), channel_id=1, source_target_pairs={{0,1},{1,0},{2,3},{3,2},{4,5},{5,4},{6,7},{7,6},{8,9},{9,8},{10,11... | collective-permute-start | bytes 196616 | tf_op jit(solution)/shard_map/ppermute | solution.py:172
  310.0 16.1 %collective-permute-start.29 = (bf16[1,128,256]{2,1,0:T(8,128)(2,1)S(1)}, bf16[1,128,256]{2,1,0:T(8,128)(2,1)S(1)}, u32[]{:S(2)}, u32[]{:S(2)}) collective-permute-start(bf16[1,128,256]{2,1,0:T(8,128)(2,1)S(1)} %get-tuple-element.101), channel_id=1, source_target_pairs={{0,2},{1,3},{2,0},{3,1},{4,6},{5,7},{6,4},{7,5},{8,10},{9,11},{10,... | collective-permute-start | bytes 196616 | tf_op jit(solution)/shard_map/ppermute | solution.py:172
  321.8 118.7 %collective-permute-start.14 = (bf16[16,256,128]{2,1,0:T(8,128)(2,1)S(1)}, bf16[16,256,128]{2,1,0:T(8,128)(2,1)S(1)}, u32[]{:S(2)}, u32[]{:S(2)}) collective-permute-start(bf16[16,256,128]{2,1,0:T(8,128)(2,1)S(1)} %get-tuple-element.83), channel_id=1, source_target_pairs={{0,1},{1,0},{2,3},{3,2},{4,5},{5,4},{6,7},{7,6},{8,9},{9,8},{10,11... | collective-permute-start | bytes 3145736 | tf_op jit(solution)/shard_map/ppermute | solution.py:172
  321.9 120.3 %collective-permute-start.15 = (bf16[16,256,128]{2,1,0:T(8,128)(2,1)S(1)}, bf16[16,256,128]{2,1,0:T(8,128)(2,1)S(1)}, u32[]{:S(2)}, u32[]{:S(2)}) collective-permute-start(bf16[16,256,128]{2,1,0:T(8,128)(2,1)S(1)} %get-tuple-element.84), channel_id=1, source_target_pairs={{0,2},{1,3},{2,0},{3,1},{4,6},{5,7},{6,4},{7,5},{8,10},{9,11},{10,... | collective-permute-start | bytes 3145736 | tf_op jit(solution)/shard_map/ppermute | solution.py:172
  326.1 39.6 %collective-permute-start.7 = (bf16[3,256,128]{2,1,0:T(8,128)(2,1)S(1)}, bf16[3,256,128]{2,1,0:T(8,128)(2,1)S(1)}, u32[]{:S(2)}, u32[]{:S(2)}) collective-permute-start(bf16[3,256,128]{2,1,0:T(8,128)(2,1)S(1)} %get-tuple-element.70), channel_id=1, source_target_pairs={{0,1},{1,0},{2,3},{3,2},{4,5},{5,4},{6,7},{7,6},{8,9},{9,8},{10,11... | collective-permute-start | bytes 589832 | tf_op jit(solution)/shard_map/ppermute | solution.py:172
  326.3 42.0 %collective-permute-start.8 = (bf16[3,256,128]{2,1,0:T(8,128)(2,1)S(1)}, bf16[3,256,128]{2,1,0:T(8,128)(2,1)S(1)}, u32[]{:S(2)}, u32[]{:S(2)}) collective-permute-start(bf16[3,256,128]{2,1,0:T(8,128)(2,1)S(1)} %get-tuple-element.71), channel_id=1, source_target_pairs={{0,2},{1,3},{2,0},{3,1},{4,6},{5,7},{6,4},{7,5},{8,10},{9,11},{10,... | collective-permute-start | bytes 589832 | tf_op jit(solution)/shard_map/ppermute | solution.py:172
  328.0 23.9 %collective-permute-start.1 = (bf16[1,256,128]{2,1,0:T(8,128)(2,1)S(1)}, bf16[1,256,128]{2,1,0:T(8,128)(2,1)S(1)}, u32[]{:S(2)}, u32[]{:S(2)}) collective-permute-start(bf16[1,256,128]{2,1,0:T(8,128)(2,1)S(1)} %get-tuple-element.63), channel_id=1, source_target_pairs={{0,2},{1,3},{2,0},{3,1},{4,6},{5,7},{6,4},{7,5},{8,10},{9,11},{10,... | collective-permute-start | bytes 196616 | tf_op jit(solution)/shard_map/ppermute | solution.py:172
  365.7 20.0 %collective-permute-start.10 = (bf16[3,256,128]{2,1,0:T(8,128)(2,1)S(1)}, bf16[3,256,128]{2,1,0:T(8,128)(2,1)S(1)}, u32[]{:S(2)}, u32[]{:S(2)}) collective-permute-start(bf16[3,256,128]{2,1,0:T(8,128)(2,1)S(1)} %get-tuple-element.73), channel_id=1, source_target_pairs={{0,4},{1,5},{2,6},{3,7},{4,0},{5,1},{6,2},{7,3},{8,12},{9,13},{10,... | collective-permute-start | bytes 589832 | tf_op jit(solution)/shard_map/ppermute | solution.py:172
  368.3 21.5 %collective-permute-start.11 = (bf16[3,256,128]{2,1,0:T(8,128)(2,1)S(1)}, bf16[3,256,128]{2,1,0:T(8,128)(2,1)S(1)}, u32[]{:S(2)}, u32[]{:S(2)}) collective-permute-start(bf16[3,256,128]{2,1,0:T(8,128)(2,1)S(1)} %get-tuple-element.74), channel_id=1, source_target_pairs={{0,5},{1,4},{2,7},{3,6},{4,1},{5,0},{6,3},{7,2},{8,13},{9,12},{10,... | collective-permute-start | bytes 589832 | tf_op jit(solution)/shard_map/ppermute | solution.py:172
  374.4 24.4 %collective-permute-start.12 = (bf16[3,256,128]{2,1,0:T(8,128)(2,1)S(1)}, bf16[3,256,128]{2,1,0:T(8,128)(2,1)S(1)}, u32[]{:S(2)}, u32[]{:S(2)}) collective-permute-start(bf16[3,256,128]{2,1,0:T(8,128)(2,1)S(1)} %get-tuple-element.75), channel_id=1, source_target_pairs={{0,6},{1,7},{2,4},{3,5},{4,2},{5,3},{6,0},{7,1},{8,14},{9,15},{10,... | collective-permute-start | bytes 589832 | tf_op jit(solution)/shard_map/ppermute | solution.py:172
  385.6 16.4 %collective-permute-start.13 = (bf16[3,256,128]{2,1,0:T(8,128)(2,1)S(1)}, bf16[3,256,128]{2,1,0:T(8,128)(2,1)S(1)}, u32[]{:S(2)}, u32[]{:S(2)}) collective-permute-start(bf16[3,256,128]{2,1,0:T(8,128)(2,1)S(1)} %get-tuple-element.76), channel_id=1, source_target_pairs={{0,7},{1,6},{2,5},{3,4},{4,3},{5,2},{6,1},{7,0},{8,15},{9,14},{10,... | collective-permute-start | bytes 589832 | tf_op jit(solution)/shard_map/ppermute | solution.py:172
  402.0 21.0 %collective-permute-start.24 = (bf16[3,128,256]{2,1,0:T(8,128)(2,1)S(1)}, bf16[3,128,256]{2,1,0:T(8,128)(2,1)S(1)}, u32[]{:S(2)}, u32[]{:S(2)}) collective-permute-start(bf16[3,128,256]{2,1,0:T(8,128)(2,1)S(1)} %get-tuple-element.95), channel_id=1, source_target_pairs={{0,4},{1,5},{2,6},{3,7},{4,0},{5,1},{6,2},{7,3},{8,12},{9,13},{10,... | collective-permute-start | bytes 589832 | tf_op jit(solution)/shard_map/ppermute | solution.py:172
  405.7 21.5 %collective-permute-start.25 = (bf16[3,128,256]{2,1,0:T(8,128)(2,1)S(1)}, bf16[3,128,256]{2,1,0:T(8,128)(2,1)S(1)}, u32[]{:S(2)}, u32[]{:S(2)}) collective-permute-start(bf16[3,128,256]{2,1,0:T(8,128)(2,1)S(1)} %get-tuple-element.96), channel_id=1, source_target_pairs={{0,5},{1,4},{2,7},{3,6},{4,1},{5,0},{6,3},{7,2},{8,13},{9,12},{10,... | collective-permute-start | bytes 589832 | tf_op jit(solution)/shard_map/ppermute | solution.py:172
  409.4 26.6 %collective-permute-start.26 = (bf16[3,128,256]{2,1,0:T(8,128)(2,1)S(1)}, bf16[3,128,256]{2,1,0:T(8,128)(2,1)S(1)}, u32[]{:S(2)}, u32[]{:S(2)}) collective-permute-start(bf16[3,128,256]{2,1,0:T(8,128)(2,1)S(1)} %get-tuple-element.97), channel_id=1, source_target_pairs={{0,6},{1,7},{2,4},{3,5},{4,2},{5,3},{6,0},{7,1},{8,14},{9,15},{10,... | collective-permute-start | bytes 589832 | tf_op jit(solution)/shard_map/ppermute | solution.py:172
  423.0 17.5 %collective-permute-start.27 = (bf16[3,128,256]{2,1,0:T(8,128)(2,1)S(1)}, bf16[3,128,256]{2,1,0:T(8,128)(2,1)S(1)}, u32[]{:S(2)}, u32[]{:S(2)}) collective-permute-start(bf16[3,128,256]{2,1,0:T(8,128)(2,1)S(1)} %get-tuple-element.98), channel_id=1, source_target_pairs={{0,7},{1,6},{2,5},{3,4},{4,3},{5,2},{6,1},{7,0},{8,15},{9,14},{10,... | collective-permute-start | bytes 589832 | tf_op jit(solution)/shard_map/ppermute | solution.py:172
  427.2 43.0 %collective-permute-start.16 = (bf16[16,256,128]{2,1,0:T(8,128)(2,1)S(1)}, bf16[16,256,128]{2,1,0:T(8,128)(2,1)S(1)}, u32[]{:S(2)}, u32[]{:S(2)}) collective-permute-start(bf16[16,256,128]{2,1,0:T(8,128)(2,1)S(1)} %get-tuple-element.85), channel_id=1, source_target_pairs={{0,3},{1,2},{2,1},{3,0},{4,7},{5,6},{6,5},{7,4},{8,11},{9,10},{10,... | collective-permute-start | bytes 3145736 | tf_op jit(solution)/shard_map/ppermute | solution.py:172
  436.0 116.3 %collective-permute-start.17 = (bf16[16,256,128]{2,1,0:T(8,128)(2,1)S(1)}, bf16[16,256,128]{2,1,0:T(8,128)(2,1)S(1)}, u32[]{:S(2)}, u32[]{:S(2)}) collective-permute-start(bf16[16,256,128]{2,1,0:T(8,128)(2,1)S(1)} %get-tuple-element.86), channel_id=1, source_target_pairs={{0,4},{1,5},{2,6},{3,7},{4,0},{5,1},{6,2},{7,3},{8,12},{9,13},{10,... | collective-permute-start | bytes 3145736 | tf_op jit(solution)/shard_map/ppermute | solution.py:172
  440.5 135.6 %collective-permute-start.18 = (bf16[16,256,128]{2,1,0:T(8,128)(2,1)S(1)}, bf16[16,256,128]{2,1,0:T(8,128)(2,1)S(1)}, u32[]{:S(2)}, u32[]{:S(2)}) collective-permute-start(bf16[16,256,128]{2,1,0:T(8,128)(2,1)S(1)} %get-tuple-element.87), channel_id=1, source_target_pairs={{0,5},{1,4},{2,7},{3,6},{4,1},{5,0},{6,3},{7,2},{8,13},{9,12},{10,... | collective-permute-start | bytes 3145736 | tf_op jit(solution)/shard_map/ppermute | solution.py:172
  440.5 162.6 %collective-permute-start.19 = (bf16[16,256,128]{2,1,0:T(8,128)(2,1)S(1)}, bf16[16,256,128]{2,1,0:T(8,128)(2,1)S(1)}, u32[]{:S(2)}, u32[]{:S(2)}) collective-permute-start(bf16[16,256,128]{2,1,0:T(8,128)(2,1)S(1)} %copy-done.5), channel_id=1, source_target_pairs={{0,6},{1,7},{2,4},{3,5},{4,2},{5,3},{6,0},{7,1},{8,14},{9,15},{10,... | collective-permute-start | bytes 3145736 | tf_op jit(solution)/shard_map/ppermute | solution.py:172
  442.3 183.4 %collective-permute-start.20 = (bf16[16,256,128]{2,1,0:T(8,128)(2,1)S(1)}, bf16[16,256,128]{2,1,0:T(8,128)(2,1)S(1)}, u32[]{:S(2)}, u32[]{:S(2)}) collective-permute-start(bf16[16,256,128]{2,1,0:T(8,128)(2,1)S(1)} %copy-done.4), channel_id=1, source_target_pairs={{0,7},{1,6},{2,5},{3,4},{4,3},{5,2},{6,1},{7,0},{8,15},{9,14},{10,... | collective-permute-start | bytes 3145736 | tf_op jit(solution)/shard_map/ppermute | solution.py:172
  470.2 184.5 %collective-permute-start.2 = (bf16[1,256,128]{2,1,0:T(8,128)(2,1)S(1)}, bf16[1,256,128]{2,1,0:T(8,128)(2,1)S(1)}, u32[]{:S(2)}, u32[]{:S(2)}) collective-permute-start(bf16[1,256,128]{2,1,0:T(8,128)(2,1)S(1)} %get-tuple-element.64), channel_id=1, source_target_pairs={{0,3},{1,2},{2,1},{3,0},{4,7},{5,6},{6,5},{7,4},{8,11},{9,10},{10,... | collective-permute-start | bytes 196616 | tf_op jit(solution)/shard_map/ppermute | solution.py:172
  552.2 102.4 %collective-permute-start.3 = (bf16[1,256,128]{2,1,0:T(8,128)(2,1)S(1)}, bf16[1,256,128]{2,1,0:T(8,128)(2,1)S(1)}, u32[]{:S(2)}, u32[]{:S(2)}) collective-permute-start(bf16[1,256,128]{2,1,0:T(8,128)(2,1)S(1)} %get-tuple-element.65), channel_id=1, source_target_pairs={{0,4},{1,5},{2,6},{3,7},{4,0},{5,1},{6,2},{7,3},{8,12},{9,13},{10,... | collective-permute-start | bytes 196616 | tf_op jit(solution)/shard_map/ppermute | solution.py:172
  576.1 78.5 %collective-permute-start.4 = (bf16[1,256,128]{2,1,0:T(8,128)(2,1)S(1)}, bf16[1,256,128]{2,1,0:T(8,128)(2,1)S(1)}, u32[]{:S(2)}, u32[]{:S(2)}) collective-permute-start(bf16[1,256,128]{2,1,0:T(8,128)(2,1)S(1)} %get-tuple-element.66), channel_id=1, source_target_pairs={{0,5},{1,4},{2,7},{3,6},{4,1},{5,0},{6,3},{7,2},{8,13},{9,12},{10,... | collective-permute-start | bytes 196616 | tf_op jit(solution)/shard_map/ppermute | solution.py:172
  603.2 51.5 %collective-permute-start.5 = (bf16[1,256,128]{2,1,0:T(8,128)(2,1)S(1)}, bf16[1,256,128]{2,1,0:T(8,128)(2,1)S(1)}, u32[]{:S(2)}, u32[]{:S(2)}) collective-permute-start(bf16[1,256,128]{2,1,0:T(8,128)(2,1)S(1)} %get-tuple-element.67), channel_id=1, source_target_pairs={{0,6},{1,7},{2,4},{3,5},{4,2},{5,3},{6,0},{7,1},{8,14},{9,15},{10,... | collective-permute-start | bytes 196616 | tf_op jit(solution)/shard_map/ppermute | solution.py:172
  625.6 29.0 %collective-permute-start.6 = (bf16[1,256,128]{2,1,0:T(8,128)(2,1)S(1)}, bf16[1,256,128]{2,1,0:T(8,128)(2,1)S(1)}, u32[]{:S(2)}, u32[]{:S(2)}) collective-permute-start(bf16[1,256,128]{2,1,0:T(8,128)(2,1)S(1)} %get-tuple-element.68), channel_id=1, source_target_pairs={{0,7},{1,6},{2,5},{3,4},{4,3},{5,2},{6,1},{7,0},{8,15},{9,14},{10,... | collective-permute-start | bytes 196616 | tf_op jit(solution)/shard_map/ppermute | solution.py:172
  (21 other events, 538.3 us)
